TPU v7x, 32 devices: a whole 2x2x4 slice. The times are simulated.
32 devices in a mesh: tower: 2 (over x), blk: 16 (over z, y, core).
Axes of the slice: x: 2, y: 2, z: 4, core: 2. Of those that a mesh axis runs over, the one named last changes fastest.
Arguments:
- pooled: bfloat16 [2, 2048, 1152], P('tower', 'blk'), may hold values from -6 to 6
- final_gain: float32 [2, 1152], P('tower'), may hold values from 0.5 to 1.5
- head_weight: bfloat16 [2, 1152, 1152], P('tower'), may hold values from -0.1875 to 0.1875
- pair_ids: int32 [2048], replicated, may hold values from 0 to 2047
- log_scale: float32 [1], replicated, may hold values from 4.2 to 4.7
- bias: float32 [1], replicated, may hold values from -4 to -1
Outputs:
- emb_grad: float32 [2, 2048, 1152], P('tower', 'blk')
Inputs may be any that keep to these rules, and one draw needn't show every extreme that they name: `pair_ids`: examples with equal ids form positive pairs; every example is a positive pair with its own image and text.
All inputs are finite; a program needn't handle non-finite values.
Results may differ from a plain program's by a relative error of at most 0.0043.
Values may be sent and summed in bfloat16 or wider, within the bound.
A program may use at most 192 MiB of HBM per device.

v0:
```python
import jax
import jax.numpy as jnp
from jax import lax
from jax.sharding import PartitionSpec as P


def partner(value, axis, stride):
    mask = 2**stride
    pairs = [(source, source ^ mask) for source in range(lax.axis_size(axis))]
    return lax.ppermute(value, axis, pairs)


def embed_rows(feats, gain, weight):
    values = feats.astype(jnp.float32)
    center = values - jnp.mean(values, axis=-1, keepdims=True)
    spread = jnp.mean(center * center, axis=-1, keepdims=True)
    normed = (center * lax.rsqrt(spread + 1e-06) * gain).astype(jnp.bfloat16)
    head = jnp.dot(normed, weight, preferred_element_type=jnp.float32)
    length = jnp.sum(head * head, axis=-1, keepdims=True)
    return (head * lax.rsqrt(length + 1e-06)).astype(jnp.bfloat16)


def pair_coef(fixed_rows, moving_rows, fixed_ids, moving_ids, scale, shift):
    logits = (
        scale
        * lax.dot_general(
            fixed_rows, moving_rows, (((1,), (1,)), ((), ())), preferred_element_type=jnp.float32
        )
        + shift
    )
    sign = jnp.where(fixed_ids[:, None] == moving_ids[None, :], jnp.float32(1.0), jnp.float32(-1.0))
    return (-sign * jax.nn.sigmoid(-sign * logits)).astype(jnp.bfloat16)


def pair_forces(fixed_rows, moving_rows, fixed_ids, moving_ids, scale, shift):
    coef = pair_coef(fixed_rows, moving_rows, fixed_ids, moving_ids, scale, shift)
    return jnp.dot(coef, moving_rows, preferred_element_type=jnp.float32)


def on_device(pooled, final_gain, head_weight, pair_ids, log_scale, bias):
    local_embed = embed_rows(pooled[0], final_gain[0], head_weight[0])
    count = local_embed.shape[0]
    scale = jnp.exp(log_scale[0])
    shift = bias[0]
    block_index = lax.axis_index("blk")
    local_ids = lax.dynamic_slice_in_dim(pair_ids, block_index * count, count)
    partner_embed = partner(local_embed, "tower", 0)
    total = pair_forces(
        local_embed,
        lax.all_gather(partner_embed, "blk", axis=0, tiled=True),
        local_ids,
        pair_ids,
        scale,
        shift,
    )
    return total[None]


def solution(mesh):
    placed = (P("tower", "blk", None), P("tower", None), P("tower", None, None), P(), P(), P())
    return jax.shard_map(
        on_device, mesh=mesh, in_specs=placed, out_specs=P("tower", "blk", None), check_vma=False
    )
```

profile of v0, /device:TPU:1, one launch (start us, length us, event | category | flops | bytes accessed | tf_op | source)
XLA Modules:
  0.0 90.7 jit_solution(13309167301348592470)
XLA Ops:
  6.5 0.0 copy-start
  6.5 0.0 copy-start.2
  6.5 0.0 all-gather.2.cloned.1.call-start
  6.5 1.2 %convert_reduce_fusion = f32[128]{0:T(128)S(1)} fusion(bf16[1,128,1152]{2,1,0:T(8,128)(2,1)} %param.6), kind=kLoop, calls=%fused_computation.14 | loop fusion | flops 294784 | bytes 295424 | tf_op jit(solution)/shard_map/reduce_sum | solution.py:15
  7.8 1.2 %fusion.15 = f32[128]{0:T(128)S(1)} fusion(bf16[1,128,1152]{2,1,0:T(8,128)(2,1)} %param.6, f32[128]{0:T(128)S(1)} %broadcast_multiply_fusion), kind=kLoop, calls=%fused_computation.20 | loop fusion | flops 589696 | bytes 295936 | tf_op jit(solution)/shard_map/reduce_sum | solution.py:16
  9.0 0.7 reduce.1
  9.7 0.0 copy-done
  9.7 1.7 %multiply_reduce_fusion = (f32[128]{0:T(128)S(1)}, f32[128,1152]{1,0:T(8,128)S(1)}) fusion(bf16[1,1152,1152]{2,1,0:T(8,128)(2,1)S(1)} %copy-done, bf16[1,128,1152]{2,1,0:T(8,128)(2,1)} %param.6, f32[1152]{0:T(1024)S(1)} %reduce.1, f32[128]{0:T(128)S(1)} %add_rsqrt_fusion.1, f32[128]{0:T(128)S(1)} %broadcast_multiply_fusion), kind=kOutput, calls=%fused_computation.22 | convolution fusion | flops 340770688 | bytes 3545088 | tf_op jit(solution)/shard_map/dot_general | solution.py:18
  11.4 0.1 multiply_convert_fusion
  11.5 2.1 %collective-permute-start = (bf16[128,1152]{1,0:T(8,128)(2,1)S(1)}, bf16[128,1152]{1,0:T(8,128)(2,1)S(1)}, u32[]{:S(2)}, u32[]{:S(2)}) collective-permute-start(bf16[128,1152]{1,0:T(8,128)(2,1)S(1)} %multiply_convert_fusion), channel_id=1, source_target_pairs={{0,16},{16,0},{1,17},{17,1},{2,18},{18,2},{3,19},{19,3},{4,20},{20... | collective-permute-start | bytes 884744 | tf_op jit(solution)/shard_map/ppermute | solution.py:10
  13.6 6.7 %collective-permute-done = bf16[128,1152]{1,0:T(8,128)(2,1)S(1)} collective-permute-done((bf16[128,1152]{1,0:T(8,128)(2,1)S(1)}, bf16[128,1152]{1,0:T(8,128)(2,1)S(1)}, u32[]{:S(2)}, u32[]{:S(2)}) %collective-permute-start) | collective-permute-done | bytes 294944 | tf_op jit(solution)/shard_map/ppermute | solution.py:10
  20.3 0.0 copy-start.1
  20.3 0.7 copy-done.1
  21.1 0.0 all-gather.2.cloned.1.call-update
  22.4 0.0 copy-done.2
  22.4 0.1 dynamic_slice.3
  22.5 54.3 %all-gather.2.cloned.1.call-done = bf16[2048,1152]{1,0:T(8,128)(2,1)} async-done(((bf16[128,1152]{1,0:T(8,128)(2,1)}), bf16[2048,1152]{1,0:T(8,128)(2,1)}) %all-gather.2.cloned.1.call-update) | async-done | bytes 4718608 | tf_op jit(solution)/shard_map/all_gather | solution.py:50
  76.8 7.0 %convolution_bitcast_fusion = f32[1,128,1152]{2,1,0:T(8,128)} fusion(bf16[2048,1152]{1,0:T(8,128)(2,1)} %all-gather.2.cloned.1.call-done, bf16[128,1152]{1,0:T(8,128)(2,1)S(1)} %multiply_convert_fusion, f32[]{:T(128)} %bitcast.25, f32[]{:T(128)} %bitcast, s32[2048]{0:T(1024)S(1)} %copy-done.2, s32[128]{0:T(128)S(1)} %dynamic_slice.3), kind=kOutput, calls=%fused_computation.2 | convolution fusion | flops 1210843136 | bytes 5612040 | tf_op jit(solution)/shard_map/dot_general | solution.py:37
  (3 shorter events, 0.0 us)
Async XLA Ops:
  6.5 3.2 %copy-start = (bf16[1,1152,1152]{2,1,0:T(8,128)(2,1)S(1)}, bf16[1,1152,1152]{2,1,0:T(8,128)(2,1)}, u32[]{:S(2)}) copy-start(bf16[1,1152,1152]{2,1,0:T(8,128)(2,1)} %param.8) | copy-start | bytes 7962628
  6.5 15.9 %copy-start.2 = (s32[2048]{0:T(1024)S(1)}, s32[2048]{0:T(1024)}, u32[]{:S(2)}) copy-start(s32[2048]{0:T(1024)} %param.9) | copy-start | bytes 24580
  6.5 70.3 %all-gather.2.cloned.1.call-start = ((), (), s32[]{:S(2)}) async-start(), calls=%async_computation | async-start | bytes 5013504 | tf_op jit(solution)/shard_map/all_gather | solution.py:50
  11.5 8.8 %collective-permute-start = (bf16[128,1152]{1,0:T(8,128)(2,1)S(1)}, bf16[128,1152]{1,0:T(8,128)(2,1)S(1)}, u32[]{:S(2)}, u32[]{:S(2)}) collective-permute-start(bf16[128,1152]{1,0:T(8,128)(2,1)S(1)} %multiply_convert_fusion), channel_id=1, source_target_pairs={{0,16},{16,0},{1,17},{17,1},{2,18},{18,2},{3,19},{19,3},{4,20},{20... | collective-permute-start | bytes 884744 | tf_op jit(solution)/shard_map/ppermute | solution.py:10
  20.3 0.7 copy-start.1
Sparse Core Ops, SparseCore 0:
  21.2 55.5 all-gather.1
where the time goes:
time: 91.1 us; the launch traced here: 90.7 us
  waiting for transfers between devices  61.1 us (67%)
  between operations  14.8 us (16%)
  matrix products  8.68 us (10%)
  other arithmetic  3.27 us (4%)
  starting transfers between devices  2.1 us (2%)
    all_gather x1, waiting for transfers between devices, on_device(): lax.all_gather(partner_embed, 'blk', axis=0, tiled=True)  54.3 us
    dot_general x1, matrix products, pair_forces(): return jnp.dot(coef, moving_rows, preferred_element_type=jnp.float32)  6.99 us
    ppermute x1, waiting for transfers between devices, partner(): return lax.ppermute(value, axis, pairs)  6.71 us
    ppermute x1, starting transfers between devices, partner(): return lax.ppermute(value, axis, pairs)  2.09 us
  transfers between devices with their start and end apart: 2, of which 2 were waited for; matrix products, arithmetic and copies ran while one was open for 0% of the time, Pallas kernels for 0%

commit v1 on v0

v1 whole, which is shorter than its diff:
```python
import functools

import jax
import jax.numpy as jnp
from jax import lax
from jax.experimental import pallas as pl
from jax.experimental.pallas import tpu as pltpu
from jax.sharding import PartitionSpec as P

MESH = pl.DeviceIdType.MESH


def grid_of(blocks):
    chips = blocks // 2
    across = 1
    while (2 * across) ** 2 <= chips and chips % (2 * across) == 0:
        across *= 2
    return chips // across, across


def by_distance(size):
    return [sorted(range(size), key=lambda other: (abs(other - here), other)) for here in range(size)]


def pick(table, here, step):
    value = jnp.int32(table[0][step])
    for place in range(1, len(table)):
        value = jnp.where(here == place, jnp.int32(table[place][step]), value)
    return value


def kernel(
    sizes, pooled, gain, ids, log_scale, bias, weight, out,
    held, local, weights, coef, weight_sem,
    got, sent_x, sent_up, sent_down, sent_right, sent_left, sent_core,
):
    depth, across, pieces = sizes
    rows = pooled.shape[0]
    part = rows // pieces
    tower = lax.axis_index("tower")
    mine = lax.axis_index("blk")
    core = lax.rem(mine, 2)
    chip = lax.div(mine, 2)
    y = lax.rem(chip, across)
    z = lax.div(chip, across)

    fetch = pltpu.make_async_copy(weight, weights, weight_sem)
    fetch.start()

    def at(z_to, y_to, core_to):
        return (z_to * across + y_to) * 2 + core_to

    up, down = at(z + 1, y, core), at(z - 1, y, core)
    right, left = at(z, y + 1, core), at(z, y - 1, core)
    twin = at(z, y, 1 - core)
    has_up, has_down = z < depth - 1, z > 0
    has_right, has_left = y < across - 1, y > 0

    barrier = pltpu.get_barrier_semaphore()

    def greet(tower_to, blk_to):
        pl.semaphore_signal(barrier, inc=1, device_id={"tower": tower_to, "blk": blk_to}, device_id_type=MESH)

    greet(1 - tower, mine)
    greet(tower, twin)
    for there, who in ((has_up, up), (has_down, down), (has_right, right), (has_left, left)):
        pl.when(there)(functools.partial(greet, tower, who))

    values = pooled[...].astype(jnp.float32)
    center = values - jnp.mean(values, axis=-1, keepdims=True)
    spread = jnp.mean(center * center, axis=-1, keepdims=True)
    normed = (center * lax.rsqrt(spread + 1e-06) * gain[...]).astype(jnp.bfloat16)
    fetch.wait()
    head = jnp.dot(normed, weights[...], preferred_element_type=jnp.float32)
    length = jnp.sum(head * head, axis=-1, keepdims=True)
    local[...] = (head * lax.rsqrt(length + 1e-06)).astype(jnp.bfloat16)

    count = (
        2
        + has_up.astype(jnp.int32)
        + has_down.astype(jnp.int32)
        + has_right.astype(jnp.int32)
        + has_left.astype(jnp.int32)
    )
    pl.semaphore_wait(barrier, count)

    def span(k):
        return pl.ds(k * part, part)

    def cross(k):
        return pltpu.make_async_remote_copy(
            src_ref=local.at[span(k)],
            dst_ref=held.at[mine, span(k)],
            send_sem=sent_x.at[k],
            recv_sem=got.at[mine, k],
            device_id={"tower": 1 - tower, "blk": mine},
            device_id_type=MESH,
        )

    def relay(block, k, sem, who):
        return pltpu.make_async_remote_copy(
            src_ref=held.at[block, span(k)],
            dst_ref=held.at[block, span(k)],
            send_sem=sem,
            recv_sem=got.at[block, k],
            device_id={"tower": tower, "blk": who},
            device_id_type=MESH,
        )

    for k in range(pieces):
        cross(k).start()

    z_table, y_table = by_distance(depth), by_distance(across)
    z_at = [pick(z_table, z, j) for j in range(depth)]
    y_at = [pick(y_table, y, i) for i in range(across)]

    def sends(j, i, k):
        z_from, y_from = z_at[j], y_at[i]
        block = at(z_from, y_from, core)
        found = [(None, relay(block, k, sent_core.at[j, i, k], twin))]
        if i == 0:
            found.append((has_up & (z_from <= z), relay(block, k, sent_up.at[j, k], up)))
            found.append((has_down & (z_from >= z), relay(block, k, sent_down.at[j, k], down)))
        found.append((has_right & (y_from <= y), relay(block, k, sent_right.at[j, i, k], right)))
        found.append((has_left & (y_from >= y), relay(block, k, sent_left.at[j, i, k], left)))
        return found[1:] + found[:1]

    def arrive(j, i, k):
        block = at(z_at[j], y_at[i], core)
        relay(block, k, sent_core.at[j, i, k], twin).wait_recv()
        for there, copy in sends(j, i, k):
            if there is None:
                copy.start()
            else:
                pl.when(there)(copy.start)

    scale = jnp.exp(jnp.full((1, rows), log_scale[0], jnp.float32))
    shift = bias[0]
    own_ids = jnp.transpose(jnp.broadcast_to(ids[pl.ds(mine, 1), :], (rows, rows)))
    out[...] = jnp.zeros_like(out)

    def forces(j, i):
        group = z_at[j] * across + y_at[i]
        other = 2 * group + 1 - core
        for k in range(pieces):
            relay(other, k, sent_core.at[j, i, k], twin).wait_recv()
        moving = held[pl.ds(2 * group, 2)].reshape(2 * rows, -1)
        dots = lax.dot_general(
            local[...], moving, (((1,), (1,)), ((), ())), preferred_element_type=jnp.float32
        )
        for half in range(2):
            logits = scale * dots[:, half * rows : (half + 1) * rows] + shift
            same = own_ids == ids[pl.ds(2 * group + half, 1), :]
            sign = jnp.where(same, jnp.float32(1.0), jnp.float32(-1.0))
            coef[:, half * rows : (half + 1) * rows] = (
                -sign / (1.0 + jnp.exp(sign * logits))
            ).astype(jnp.bfloat16)
        out[...] += jnp.dot(coef[...], moving, preferred_element_type=jnp.float32)

    waiting = []
    for wave in range(depth + across - 1):
        fresh = [(j, wave - j) for j in range(depth) if 0 <= wave - j < across]
        fresh.sort(key=lambda pair: pair[1])
        for k in range(pieces):
            for j, i in fresh:
                arrive(j, i, k)
            if waiting:
                forces(*waiting.pop(0))
        waiting += fresh
    for pair in waiting:
        forces(*pair)

    for k in range(pieces):
        cross(k).wait_send()
    for j in range(depth):
        for i in range(across):
            for k in range(pieces):
                for there, copy in sends(j, i, k):
                    if there is None:
                        copy.wait_send()
                    else:
                        pl.when(there)(copy.wait_send)


def solution(mesh):
    blocks = mesh.shape["blk"]
    depth, across = grid_of(blocks)
    pieces = 4 if blocks <= 16 else 1

    def on_device(pooled, final_gain, head_weight, pair_ids, log_scale, bias):
        _, rows, width = pooled.shape
        vmem = pl.BlockSpec(memory_space=pltpu.VMEM)
        smem = pl.BlockSpec(memory_space=pltpu.SMEM)
        dma = pltpu.SemaphoreType.DMA
        total = pl.pallas_call(
            functools.partial(kernel, (depth, across, pieces)),
            name="tower_forces",
            out_shape=jax.ShapeDtypeStruct((rows, width), jnp.float32),
            in_specs=[vmem, vmem, vmem, smem, smem, pl.BlockSpec(memory_space=pl.ANY)],
            out_specs=vmem,
            scratch_shapes=[
                pltpu.VMEM((blocks, rows, width), jnp.bfloat16),
                pltpu.VMEM((rows, width), jnp.bfloat16),
                pltpu.VMEM((width, width), jnp.bfloat16),
                pltpu.VMEM((rows, 2 * rows), jnp.bfloat16),
                dma,
                dma((blocks, pieces)),
                dma((pieces,)),
                dma((depth, pieces)),
                dma((depth, pieces)),
                dma((depth, across, pieces)),
                dma((depth, across, pieces)),
                dma((depth, across, pieces)),
            ],
            compiler_params=pltpu.CompilerParams(
                collective_id=0, has_side_effects=True, vmem_limit_bytes=60 * 2**20
            ),
        )(pooled[0], final_gain, pair_ids.reshape(blocks, rows), log_scale, bias, head_weight[0])
        return total[None]

    placed = (P("tower", "blk", None), P("tower", None), P("tower", None, None), P(), P(), P())
    return jax.shard_map(
        on_device, mesh=mesh, in_specs=placed, out_specs=P("tower", "blk", None), check_vma=False
    )
```

time: 91.1 us -> 44.8 us (0.49)
  waiting for transfers between devices: 61.1 us -> 0 us
  Pallas kernels: 0 us -> 41.4 us
  between operations: 14.8 us -> 1.3 us
  matrix products: 8.68 us -> 0 us
  other arithmetic: 3.27 us -> 0 us
  starting transfers between devices: 2.1 us -> 0 us
  local copies, waits for them, and re-layouts: 0.8 us -> 1.92 us
    all_gather x1 -> x0, waiting for transfers between devices: 54.3 us -> none  [on_device(): lax.all_gather(partner_embed, 'blk', axis=0, tiled=True)]
    pallas_call x0 -> x1, Pallas kernels: none -> 41.4 us  [on_device(): pl.pallas_call(functools.partial(kernel, (depth, across, pieces)), name='...]
    dot_general x2 -> x0, matrix products: 8.68 us -> none  [the longest x1 6.99 us: pair_forces(): return jnp.dot(coef, moving_rows, preferred_element_type=jnp.float32)]
    ppermute x1 -> x0, waiting for transfers between devices: 6.71 us -> none  [partner(): return lax.ppermute(value, axis, pairs)]
    reduce_sum x2 -> x0, other arithmetic: 2.42 us -> none  [the longest x1 1.23 us: embed_rows(): center = values - jnp.mean(values, axis=-1, keepdims=True)]
    ppermute x1 -> x0, starting transfers between devices: 2.09 us -> none  [partner(): return lax.ppermute(value, axis, pairs)]
    unnamed x6 -> x1, local copies, waits for them, and re-layouts: 0.72 us -> 1.92 us
  transfers between devices with their start and end apart: 2 -> 0, of which waited for: 2 -> 0; matrix products, arithmetic and copies ran while one was open for 0% -> 0% of each run, Pallas kernels for 0% -> 0%
where the time goes in v1:
time: 44.8 us; the launch traced here: 44.6 us
  Pallas kernels  41.4 us (92%)
  local copies, waits for them, and re-layouts  1.92 us (4%)
  between operations  1.3 us (3%)
    pallas_call x1, Pallas kernels, on_device(): pl.pallas_call(functools.partial(kernel, (depth, across, pieces)), name='...  41.4 us
    unnamed x1, local copies, waits for them, and re-layouts  1.92 us

profile of v1, /device:TPU:1, one launch (start us, length us, event | category | flops | bytes accessed | tf_op | source)
XLA Modules:
  0.0 44.6 jit_solution(2308814316851948786)
XLA Ops:
  1.3 41.4 %tower_forces.1 = f32[128,1152]{1,0:T(8,128)} custom-call(bf16[128,1152]{1,0:T(8,128)(2,1)} %bitcast.6, f32[1,1152]{1,0:T(1,128)} %gain.1, s32[16,128]{1,0:T(8,128)} %bitcast.7, f32[1]{0:T(128)S(6)} %copy.8.log_scale, f32[1]{0:T(128)S(6)} %copy.9.bias, bf16[1152,1152]{1,0:T(8,128)(2,1)} %bitcast.4), custom_call_target="tpu_custom_call" | custom-call | tf_op jit(solution)/shard_map/tower_forces/pallas_call | solution.py:195
  42.7 1.9 %copy.10 = f32[1,128,1152]{2,1,0:T(8,128)} copy(f32[1,128,1152]{2,1,0:T(8,128)} %bitcast.5) | data formatting | bytes 1179648

commit v2 on v1

--- a/solution.py
+++ b/solution.py
@@ -30,12 +30,15 @@
 
 
 def kernel(
-    sizes, pooled, gain, ids, log_scale, bias, weight, out,
-    held, local, weights, coef, weight_sem,
-    got, sent_x, sent_up, sent_down, sent_right, sent_left, sent_core,
+    sizes, log_scale, bias, pooled_hbm, gain_hbm, ids_hbm, weight, out,
+    held, local, near, pooled, gain, ids, weights, head, coef, fetch_sem, weight_sem,
+    got, near_got, sent_x, sent_near, sent_over, sent_level,
+    sent_up, sent_down, sent_right, sent_left, sent_core,
 ):
     depth, across, pieces = sizes
-    rows = pooled.shape[0]
+    swap = across == 2
+    level = swap and pieces > 1 and depth % 2 == 0
+    rows, width = pooled.shape
     part = rows // pieces
     tower = lax.axis_index("tower")
     mine = lax.axis_index("blk")
@@ -44,8 +47,21 @@
     y = lax.rem(chip, across)
     z = lax.div(chip, across)
 
-    fetch = pltpu.make_async_copy(weight, weights, weight_sem)
-    fetch.start()
+    fetches = [
+        pltpu.make_async_copy(pooled_hbm, pooled, fetch_sem.at[0]),
+        pltpu.make_async_copy(gain_hbm, gain, fetch_sem.at[1]),
+        pltpu.make_async_copy(ids_hbm, ids, fetch_sem.at[2]),
+    ]
+    for fetch in fetches:
+        fetch.start()
+    slices = weight_sem.shape[0]
+    columns = [pl.ds(s * (width // slices), width // slices) for s in range(slices)]
+    weight_fetches = [
+        pltpu.make_async_copy(weight.at[:, columns[s]], weights.at[:, columns[s]], weight_sem.at[s])
+        for s in range(slices)
+    ]
+    for fetch in weight_fetches:
+        fetch.start()
 
     def at(z_to, y_to, core_to):
         return (z_to * across + y_to) * 2 + core_to
@@ -66,14 +82,19 @@
     for there, who in ((has_up, up), (has_down, down), (has_right, right), (has_left, left)):
         pl.when(there)(functools.partial(greet, tower, who))
 
+    fetches[0].wait()
+    fetches[1].wait()
     values = pooled[...].astype(jnp.float32)
     center = values - jnp.mean(values, axis=-1, keepdims=True)
     spread = jnp.mean(center * center, axis=-1, keepdims=True)
     normed = (center * lax.rsqrt(spread + 1e-06) * gain[...]).astype(jnp.bfloat16)
-    fetch.wait()
-    head = jnp.dot(normed, weights[...], preferred_element_type=jnp.float32)
-    length = jnp.sum(head * head, axis=-1, keepdims=True)
-    local[...] = (head * lax.rsqrt(length + 1e-06)).astype(jnp.bfloat16)
+    length = jnp.zeros((rows, 1), jnp.float32)
+    for s in range(slices):
+        weight_fetches[s].wait()
+        piece = jnp.dot(normed, weights[:, columns[s]], preferred_element_type=jnp.float32)
+        length += jnp.sum(piece * piece, axis=-1, keepdims=True)
+        head[:, columns[s]] = piece
+    local[...] = (head[...] * lax.rsqrt(length + 1e-06)).astype(jnp.bfloat16)
 
     count = (
         2
@@ -107,8 +128,37 @@
             device_id_type=MESH,
         )
 
+    beside = at(z, 1 - y, core)
+
+    def step_near(k):
+        return pltpu.make_async_remote_copy(
+            src_ref=local.at[span(k)],
+            dst_ref=near.at[span(k)],
+            send_sem=sent_near.at[k],
+            recv_sem=near_got.at[k],
+            device_id={"tower": tower, "blk": beside},
+            device_id_type=MESH,
+        )
+
+    def step_over(k):
+        return pltpu.make_async_remote_copy(
+            src_ref=near.at[span(k)],
+            dst_ref=held.at[beside, span(k)],
+            send_sem=sent_over.at[k],
+            recv_sem=got.at[beside, k],
+            device_id={"tower": 1 - tower, "blk": mine},
+            device_id_type=MESH,
+        )
+
+    pair_z = z + 1 - 2 * lax.rem(z, 2)
+
+    def step_level():
+        return relay(beside, pieces - 1, sent_level.at[0], at(pair_z, y, core))
+
     for k in range(pieces):
         cross(k).start()
+        if swap:
+            step_near(k).start()
 
     z_table, y_table = by_distance(depth), by_distance(across)
     z_at = [pick(z_table, z, j) for j in range(depth)]
@@ -121,8 +171,14 @@
         if i == 0:
             found.append((has_up & (z_from <= z), relay(block, k, sent_up.at[j, k], up)))
             found.append((has_down & (z_from >= z), relay(block, k, sent_down.at[j, k], down)))
-        found.append((has_right & (y_from <= y), relay(block, k, sent_right.at[j, i, k], right)))
-        found.append((has_left & (y_from >= y), relay(block, k, sent_left.at[j, i, k], left)))
+        if not (swap and j == 0):
+            over = True
+            if level and i == 0 and k == pieces - 1:
+                over = z_from != pair_z
+            found.append((has_right & (y_from <= y) & over, relay(block, k, sent_right.at[j, i, k], right)))
+            found.append((has_left & (y_from >= y) & over, relay(block, k, sent_left.at[j, i, k], left)))
+        if level and j == 0 and i == 1 and k == pieces - 1:
+            found.append((None, step_level()))
         return found[1:] + found[:1]
 
     def arrive(j, i, k):
@@ -134,6 +190,7 @@
             else:
                 pl.when(there)(copy.start)
 
+    fetches[2].wait()
     scale = jnp.exp(jnp.full((1, rows), log_scale[0], jnp.float32))
     shift = bias[0]
     own_ids = jnp.transpose(jnp.broadcast_to(ids[pl.ds(mine, 1), :], (rows, rows)))
@@ -162,6 +219,9 @@
         fresh = [(j, wave - j) for j in range(depth) if 0 <= wave - j < across]
         fresh.sort(key=lambda pair: pair[1])
         for k in range(pieces):
+            if swap and wave == 0:
+                step_near(k).wait_recv()
+                step_over(k).start()
             for j, i in fresh:
                 arrive(j, i, k)
             if waiting:
@@ -172,6 +232,9 @@
 
     for k in range(pieces):
         cross(k).wait_send()
+        if swap:
+            step_near(k).wait_send()
+            step_over(k).wait_send()
     for j in range(depth):
         for i in range(across):
             for k in range(pieces):
@@ -189,23 +252,35 @@
 
     def on_device(pooled, final_gain, head_weight, pair_ids, log_scale, bias):
         _, rows, width = pooled.shape
-        vmem = pl.BlockSpec(memory_space=pltpu.VMEM)
         smem = pl.BlockSpec(memory_space=pltpu.SMEM)
+        hbm = pl.BlockSpec(memory_space=pltpu.HBM)
         dma = pltpu.SemaphoreType.DMA
+        slices = 3 if width % 384 == 0 else 1
+        grant = 67043328 - 4 * rows * width - 2**17
         total = pl.pallas_call(
             functools.partial(kernel, (depth, across, pieces)),
             name="tower_forces",
-            out_shape=jax.ShapeDtypeStruct((rows, width), jnp.float32),
-            in_specs=[vmem, vmem, vmem, smem, smem, pl.BlockSpec(memory_space=pl.ANY)],
-            out_specs=vmem,
+            out_shape=pltpu.VMEM((rows, width), jnp.float32),
+            in_specs=[smem, smem, hbm, hbm, hbm, hbm],
+            out_specs=pl.BlockSpec(memory_space=pltpu.VMEM),
             scratch_shapes=[
                 pltpu.VMEM((blocks, rows, width), jnp.bfloat16),
                 pltpu.VMEM((rows, width), jnp.bfloat16),
+                pltpu.VMEM((rows, width), jnp.bfloat16),
+                pltpu.VMEM((rows, width), jnp.bfloat16),
+                pltpu.VMEM((1, width), jnp.float32),
+                pltpu.VMEM((blocks, rows), jnp.int32),
                 pltpu.VMEM((width, width), jnp.bfloat16),
+                pltpu.VMEM((rows, width), jnp.float32),
                 pltpu.VMEM((rows, 2 * rows), jnp.bfloat16),
-                dma,
+                dma((3,)),
+                dma((slices,)),
                 dma((blocks, pieces)),
                 dma((pieces,)),
+                dma((pieces,)),
+                dma((pieces,)),
+                dma((pieces,)),
+                dma((1,)),
                 dma((depth, pieces)),
                 dma((depth, pieces)),
                 dma((depth, across, pieces)),
@@ -213,9 +288,9 @@
                 dma((depth, across, pieces)),
             ],
             compiler_params=pltpu.CompilerParams(
-                collective_id=0, has_side_effects=True, vmem_limit_bytes=60 * 2**20
+                collective_id=0, has_side_effects=True, vmem_limit_bytes=grant
             ),
-        )(pooled[0], final_gain, pair_ids.reshape(blocks, rows), log_scale, bias, head_weight[0])
+        )(log_scale, bias, pooled[0], final_gain, pair_ids.reshape(blocks, rows), head_weight[0])
         return total[None]
 
     placed = (P("tower", "blk", None), P("tower", None), P("tower", None, None), P(), P(), P())

time: 44.8 us -> 45.5 us (1.016)
  Pallas kernels: 41.4 us -> 43.2 us
  local copies, waits for them, and re-layouts: 1.92 us -> 0.82 us
    pallas_call x1, Pallas kernels: 41.4 us -> 43.2 us  [on_device(): pl.pallas_call(functools.partial(kernel, (depth, across, pieces)), name='...]
    unnamed x1, local copies, waits for them, and re-layouts: 1.92 us -> 0.82 us
where the time goes in v2:
time: 45.5 us; the launch traced here: 45.3 us
  Pallas kernels  43.2 us (95%)
  between operations  1.3 us (3%)
  local copies, waits for them, and re-layouts  0.82 us (2%)
    pallas_call x1, Pallas kernels, on_device(): pl.pallas_call(functools.partial(kernel, (depth, across, pieces)), name='...  43.2 us

profile of v2, /device:TPU:1, one launch (start us, length us, event | category | flops | bytes accessed | tf_op | source)
XLA Modules:
  0.0 45.3 jit_solution(7640795216331822216)
XLA Ops:
  1.3 43.2 %tower_forces.1 = f32[128,1152]{1,0:T(8,128)S(1)} custom-call(f32[1]{0:T(128)S(6)} %copy.9.log_scale, f32[1]{0:T(128)S(6)} %copy.10.bias, bf16[128,1152]{1,0:T(8,128)(2,1)} %bitcast.6, f32[1,1152]{1,0:T(1,128)} %gain_hbm.1, s32[16,128]{1,0:T(8,128)} %bitcast.7, bf16[1152,1152]{1,0:T(8,128)(2,1)} %bitcast.5), custom_call_target="tpu_custom_call" | custom-call | tf_op jit(solution)/shard_map/tower_forces/pallas_call | solution.py:260
  44.5 0.8 %copy.8 = f32[1,128,1152]{2,1,0:T(8,128)} copy(f32[1,128,1152]{2,1,0:T(8,128)S(1)} %bitcast.4) | data formatting | bytes 1179648

commit v3 on v2

--- a/solution.py
+++ b/solution.py
@@ -8,6 +8,7 @@
 from jax.sharding import PartitionSpec as P
 
 MESH = pl.DeviceIdType.MESH
+FIRST, LATER, NEAR, LAG = 11, 15, 1.5, 4
 
 
 def grid_of(blocks):
@@ -164,31 +165,64 @@
     z_at = [pick(z_table, z, j) for j in range(depth)]
     y_at = [pick(y_table, y, i) for i in range(across)]
 
-    def sends(j, i, k):
-        z_from, y_from = z_at[j], y_at[i]
+    def lines(here, size, there):
+        found = [(0, here, None)]
+        for step in range(1, size):
+            found.append((step, here - step, here >= step))
+            found.append((step, here + step, here + step < size))
+        return found
+
+    sources = [
+        (dz, dy, z_from, y_from, [test for test in (z_test, y_test) if test is not None])
+        for dz, z_from, z_test in lines(z, depth, z)
+        for dy, y_from, y_test in lines(y, across, y)
+    ]
+
+    def guarded(tests, action):
+        if tests:
+            pl.when(functools.reduce(jnp.logical_and, tests))(action)
+        else:
+            action()
+
+    def sends(source, k):
+        dz, dy, z_from, y_from, tests = source
         block = at(z_from, y_from, core)
-        found = [(None, relay(block, k, sent_core.at[j, i, k], twin))]
-        if i == 0:
-            found.append((has_up & (z_from <= z), relay(block, k, sent_up.at[j, k], up)))
-            found.append((has_down & (z_from >= z), relay(block, k, sent_down.at[j, k], down)))
-        if not (swap and j == 0):
-            over = True
-            if level and i == 0 and k == pieces - 1:
-                over = z_from != pair_z
-            found.append((has_right & (y_from <= y) & over, relay(block, k, sent_right.at[j, i, k], right)))
-            found.append((has_left & (y_from >= y) & over, relay(block, k, sent_left.at[j, i, k], left)))
-        if level and j == 0 and i == 1 and k == pieces - 1:
-            found.append((None, step_level()))
-        return found[1:] + found[:1]
-
-    def arrive(j, i, k):
-        block = at(z_at[j], y_at[i], core)
-        relay(block, k, sent_core.at[j, i, k], twin).wait_recv()
-        for there, copy in sends(j, i, k):
-            if there is None:
-                copy.start()
-            else:
-                pl.when(there)(copy.start)
+        found = []
+        if dy == 0:
+            found.append(([has_up, z_from <= z], relay(block, k, sent_up.at[z_from, k], up)))
+            found.append(([has_down, z_from >= z], relay(block, k, sent_down.at[z_from, k], down)))
+        if not (swap and (dz == 0 or dy > 0)):
+            over = []
+            if level and dz == 1 and k == pieces - 1:
+                over = [z_from != pair_z]
+            found.append(
+                ([has_right, y_from <= y] + over, relay(block, k, sent_right.at[z_from, y_from, k], right))
+            )
+            found.append(
+                ([has_left, y_from >= y] + over, relay(block, k, sent_left.at[z_from, y_from, k], left))
+            )
+        if level and dz == 0 and dy == 1 and k == pieces - 1:
+            found.append(([], step_level()))
+        found.append(([], relay(block, k, sent_core.at[z_from, y_from, k], twin)))
+        return [(tests + more, copy) for more, copy in found]
+
+    def arrive(source, k):
+        dz, dy, z_from, y_from, tests = source
+
+        def land():
+            block = at(z_from, y_from, core)
+            relay(block, k, sent_core.at[z_from, y_from, k], twin).wait_recv()
+            for more, copy in sends(source, k):
+                guarded(more[len(tests) :], copy.start)
+
+        guarded(tests, land)
+
+    def due(dz, dy, k):
+        if dy == 0:
+            return 1 + k if dz == 0 else 3 + 4 * (dz - 1) + k
+        if dz == 0:
+            return (FIRST if swap else 4) + 4 * (dy - 1) + k
+        return LATER + 4 * (dz - 1) + 4 * (dy - 1) + k
 
     fetches[2].wait()
     scale = jnp.exp(jnp.full((1, rows), log_scale[0], jnp.float32))
@@ -200,7 +234,7 @@
         group = z_at[j] * across + y_at[i]
         other = 2 * group + 1 - core
         for k in range(pieces):
-            relay(other, k, sent_core.at[j, i, k], twin).wait_recv()
+            relay(other, k, sent_core.at[0, 0, k], twin).wait_recv()
         moving = held[pl.ds(2 * group, 2)].reshape(2 * rows, -1)
         dots = lax.dot_general(
             local[...], moving, (((1,), (1,)), ((), ())), preferred_element_type=jnp.float32
@@ -214,35 +248,33 @@
             ).astype(jnp.bfloat16)
         out[...] += jnp.dot(coef[...], moving, preferred_element_type=jnp.float32)
 
-    waiting = []
-    for wave in range(depth + across - 1):
-        fresh = [(j, wave - j) for j in range(depth) if 0 <= wave - j < across]
-        fresh.sort(key=lambda pair: pair[1])
-        for k in range(pieces):
-            if swap and wave == 0:
+    events = []
+    for k in range(pieces):
+        for source in sources:
+            events.append((due(source[0], source[1], k), functools.partial(arrive, source, k)))
+        if swap:
+
+            def pass_over(k=k):
                 step_near(k).wait_recv()
                 step_over(k).start()
-            for j, i in fresh:
-                arrive(j, i, k)
-            if waiting:
-                forces(*waiting.pop(0))
-        waiting += fresh
-    for pair in waiting:
-        forces(*pair)
+
+            events.append((k + NEAR, pass_over))
+    for j in range(depth):
+        for i in range(across):
+            events.append((due(j, i, pieces - 1) + LAG, functools.partial(forces, j, i)))
+    events.sort(key=lambda event: event[0])
+    for _, action in events:
+        action()
 
     for k in range(pieces):
         cross(k).wait_send()
         if swap:
             step_near(k).wait_send()
             step_over(k).wait_send()
-    for j in range(depth):
-        for i in range(across):
-            for k in range(pieces):
-                for there, copy in sends(j, i, k):
-                    if there is None:
-                        copy.wait_send()
-                    else:
-                        pl.when(there)(copy.wait_send)
+    for source in sources:
+        for k in range(pieces):
+            for tests, copy in sends(source, k):
+                guarded(tests, copy.wait_send)
 
 
 def solution(mesh):

time: 45.5 us -> 40.4 us (0.89)
  Pallas kernels: 43.2 us -> 38.1 us
    pallas_call x1, Pallas kernels: 43.2 us -> 38.1 us  [on_device(): pl.pallas_call(functools.partial(kernel, (depth, across, pieces)), name='...]
where the time goes in v3:
time: 40.4 us; the launch traced here: 40.2 us
  Pallas kernels  38.1 us (94%)
  between operations  1.3 us (3%)
  local copies, waits for them, and re-layouts  0.82 us (2%)
    pallas_call x1, Pallas kernels, on_device(): pl.pallas_call(functools.partial(kernel, (depth, across, pieces)), name='...  38.1 us
    unnamed x1, local copies, waits for them, and re-layouts  0.82 us

profile of v3, /device:TPU:1, one launch (start us, length us, event | category | flops | bytes accessed | tf_op | source)
XLA Modules:
  0.0 40.2 jit_solution(17429645259722771617)
XLA Ops:
  1.3 38.1 %tower_forces.1 = f32[128,1152]{1,0:T(8,128)S(1)} custom-call(f32[1]{0:T(128)S(6)} %copy.9.log_scale, f32[1]{0:T(128)S(6)} %copy.10.bias, bf16[128,1152]{1,0:T(8,128)(2,1)} %bitcast.6, f32[1,1152]{1,0:T(1,128)} %gain_hbm.1, s32[16,128]{1,0:T(8,128)} %bitcast.7, bf16[1152,1152]{1,0:T(8,128)(2,1)} %bitcast.5), custom_call_target="tpu_custom_call" | custom-call | tf_op jit(solution)/shard_map/tower_forces/pallas_call | solution.py:292
  39.4 0.8 %copy.8 = f32[1,128,1152]{2,1,0:T(8,128)} copy(f32[1,128,1152]{2,1,0:T(8,128)S(1)} %bitcast.4) | data formatting | bytes 1179648
